TPU v7x, 32 devices: a whole 2x2x4 slice. The times are simulated.
32 devices in a mesh: gx: 4 (over y, core), gy: 4 (over z), gz: 2 (over x).
Axes of the slice: x: 2, y: 2, z: 4, core: 2. Of those that a mesh axis runs over, the one named last changes fastest.
Arguments:
- stream: bfloat16 [8192, 8192], P(('gx', 'gy', 'gz')), may hold values from -4 to 4
- segment_ids: int32 [8192], P(('gx', 'gy', 'gz')), may hold values from 0 to 8191, as said below
- positions: int32 [8192], P(('gx', 'gy', 'gz')), may hold values from 0 to 255, as said below
- norm_gain: bfloat16 [1, 8192], P(None, ('gx', 'gy', 'gz')), may hold values from 0.099609375 to 1.8984375
- q_weight: bfloat16 [1, 8192, 512], P(None, ('gx', 'gy', 'gz')), as said below
- k_weight: bfloat16 [1, 8192, 128], P(None, ('gx', 'gy', 'gz')), as said below
- v_weight: bfloat16 [1, 8192, 128], P(None, ('gx', 'gy', 'gz')), may hold values from -0.0625 to 0.0625
- o_weight: bfloat16 [1, 512, 8192], P(None, None, ('gx', 'gy', 'gz')), may hold values from -0.25 to 0.25
Outputs:
- result: bfloat16 [8192, 8192], P(('gx', 'gy', 'gz'))
Inputs may be any that keep to these rules, and one draw needn't show every extreme that they name: `segment_ids`: each token's id is the index of its document's first token, so ids never fall along the tokens; every document lies inside one aligned block of 256 tokens, every block starts a new document, and the last token is a document of its own. `positions`: counts from 0 at a document's first token and rises by one per token. `q_weight`: A projection scaled by its fan-in. `k_weight`: A projection scaled by its fan-in.
All inputs are finite; a program needn't handle non-finite values.
Results may differ from a plain program's by a relative error of at most 0.0064.
Values may be sent and summed in bfloat16 or wider, within the bound.
A program may use at most 128 MiB of HBM per device.

v0:
```python
import math

import jax
import jax.numpy as jnp
from jax import lax
from jax.sharding import PartitionSpec as P


def rotate(values, positions):
    width = values.shape[-1]
    half = width // 2
    freqs = jnp.exp(-math.log(500000.0) * jnp.arange(half, dtype=jnp.float32) * 2.0 / width)
    angles = positions.astype(jnp.float32)[:, None] * freqs[None, :]
    cosine = jnp.concatenate([jnp.cos(angles), jnp.cos(angles)], -1)[:, None, :]
    sine = jnp.concatenate([jnp.sin(angles), jnp.sin(angles)], -1)[:, None, :]
    turned = jnp.concatenate([-values[..., half:], values[..., :half]], -1)
    return values * cosine + turned * sine


def attend(queries, keys, values, segment_ids, positions):
    count = queries.shape[0]
    scores = jnp.einsum(
        "thd,sd->hts", queries, keys, preferred_element_type=jnp.float32
    ) / math.sqrt(keys.shape[-1])
    allowed = (segment_ids[:, None] == segment_ids[None, :]) & (
        positions[None, :] <= positions[:, None]
    )
    scores = jnp.where(allowed[None], scores, -1e30)
    peak = jnp.max(scores, -1, keepdims=True)
    expd = jnp.exp(scores - peak)
    probs = (expd / jnp.sum(expd, -1, keepdims=True)).astype(jnp.bfloat16)
    mixed = jnp.einsum("hts,sd->thd", probs, values, preferred_element_type=jnp.float32)
    return mixed.astype(jnp.bfloat16).reshape(count, -1)


def body(stream, segment_ids, positions, norm_gain, q_weight, k_weight, v_weight, o_weight):
    count = stream.shape[0]
    head_size = k_weight.shape[2]
    current = stream
    widened = lax.optimization_barrier(current).astype(jnp.float32)
    inverse = lax.rsqrt(jnp.mean(widened * widened, -1, keepdims=True) + 1e-05)
    scaled = widened * inverse
    inner = (
        lax.all_gather(norm_gain[0], "gz", axis=0, tiled=True),
        lax.all_gather(q_weight[0], "gz", axis=0, tiled=True),
        lax.all_gather(k_weight[0], "gz", axis=0, tiled=True),
        lax.all_gather(v_weight[0], "gz", axis=0, tiled=True),
    )
    middle = (
        lax.all_gather(inner[0], "gy", axis=0, tiled=True),
        lax.all_gather(inner[1], "gy", axis=0, tiled=True),
        lax.all_gather(inner[2], "gy", axis=0, tiled=True),
        lax.all_gather(inner[3], "gy", axis=0, tiled=True),
    )
    gain_piece = lax.all_gather(middle[0], "gx", axis=0, tiled=True)
    query_piece = lax.all_gather(middle[1], "gx", axis=0, tiled=True)
    key_piece = lax.all_gather(middle[2], "gx", axis=0, tiled=True)
    value_piece = lax.all_gather(middle[3], "gx", axis=0, tiled=True)
    normed = (scaled * gain_piece.astype(jnp.float32)[None, :]).astype(jnp.bfloat16)
    query_raw = jnp.dot(normed, query_piece, preferred_element_type=jnp.float32)
    key_raw = jnp.dot(normed, key_piece, preferred_element_type=jnp.float32)
    value_raw = jnp.dot(normed, value_piece, preferred_element_type=jnp.float32)
    queries = rotate(query_raw.reshape(count, -1, head_size), positions).astype(jnp.bfloat16)
    keys = rotate(key_raw[:, None, :], positions)[:, 0, :].astype(jnp.bfloat16)
    values = value_raw.astype(jnp.bfloat16)
    mixed = attend(queries, keys, values, segment_ids, positions)
    inner_cols = lax.all_gather(o_weight[0], "gz", axis=1, tiled=True)
    middle_cols = lax.all_gather(inner_cols, "gy", axis=1, tiled=True)
    branch = jnp.dot(
        mixed,
        lax.all_gather(middle_cols, "gx", axis=1, tiled=True),
        preferred_element_type=jnp.float32,
    )
    current = (widened + branch).astype(jnp.bfloat16)
    return current


def solution(mesh):
    in_specs = (
        P(("gx", "gy", "gz"), None),
        P(("gx", "gy", "gz")),
        P(("gx", "gy", "gz")),
        P(None, ("gx", "gy", "gz")),
        P(None, ("gx", "gy", "gz"), None),
        P(None, ("gx", "gy", "gz"), None),
        P(None, ("gx", "gy", "gz"), None),
        P(None, None, ("gx", "gy", "gz")),
    )
    out_specs = P(("gx", "gy", "gz"), None)
    return jax.shard_map(body, mesh=mesh, in_specs=in_specs, out_specs=out_specs, check_vma=False)
```

profile of v0, /device:TPU:1, one launch (start us, length us, event | category | flops | bytes accessed | tf_op | source)
XLA Modules:
  0.0 307.2 jit_solution(744721059821343803)
XLA Ops:
  6.5 0.0 all-gather.26.cloned.1.call-start
  6.5 10.8 %all-gather.9 = bf16[1,512,512]{2,1,0:T(8,128)(2,1)} all-gather(bf16[1,256,512]{2,1,0:T(8,128)(2,1)} %param.12), channel_id=11, replica_groups=mesh['gx'=4,'gy'=4,'gz'=2] {'gz'}, dimensions={1}, use_global_device_ids=true | all-gather | bytes 786432 | tf_op jit(solution)/shard_map/all_gather | solution.py:45
  17.3 0.0 all-gather.26.cloned.1.call-update
  17.4 0.0 copy-start.3
  17.4 0.0 copy-start.1
  17.4 0.0 all-gather.30.cloned.1.call-start
  17.4 7.6 %all-gather.12 = bf16[1,512,512]{2,1,0:T(8,128)(2,1)} all-gather(bf16[1,512,256]{2,1,0:T(8,128)(2,1)} %param.15), channel_id=14, replica_groups=mesh['gx'=4,'gy'=4,'gz'=2] {'gz'}, dimensions={2}, use_global_device_ids=true | all-gather | bytes 786432 | tf_op jit(solution)/shard_map/all_gather | solution.py:67
  25.0 0.0 all-gather.30.cloned.1.call-update
  25.1 0.0 all-gather.24.cloned.1.call-start
  25.1 5.0 %all-gather.6 = bf16[1,512,128]{2,1,0:T(8,128)(2,1)S(1)} all-gather(bf16[1,256,128]{2,1,0:T(8,128)(2,1)} %param.13), channel_id=8, replica_groups=mesh['gx'=4,'gy'=4,'gz'=2] {'gz'}, dimensions={1}, use_global_device_ids=true | all-gather | bytes 196608 | tf_op jit(solution)/shard_map/all_gather | solution.py:46
  30.1 21.2 %all-gather.7 = bf16[1,2048,128]{2,1,0:T(8,128)(2,1)} all-gather(bf16[1,512,128]{2,1,0:T(8,128)(2,1)S(1)} %all-gather.6), channel_id=9, replica_groups=mesh['gx'=4,'gy'=4,'gz'=2] {'gy'}, dimensions={1}, use_global_device_ids=true | all-gather | bytes 655360 | tf_op jit(solution)/shard_map/all_gather | solution.py:52
  51.3 0.0 all-gather.24.cloned.1.call-update
  51.3 0.0 all-gather.28.cloned.1.call-start
  51.4 20.9 %all-gather.26.cloned.1.call-done = bf16[1,2048,512]{2,1,0:T(8,128)(2,1)} async-done(((bf16[1,512,512]{2,1,0:T(8,128)(2,1)}), bf16[1,2048,512]{2,1,0:T(8,128)(2,1)}) %all-gather.26.cloned.1.call-update) | async-done | bytes 2097168 | tf_op jit(solution)/shard_map/all_gather | solution.py:51
  72.3 0.0 all-gather.28.cloned.1.call-update
  72.4 0.0 copy-start.2
  72.4 0.0 all-gather.22.cloned.1.call-start
  72.4 0.0 copy-done
  72.4 3.8 %all-gather.3 = bf16[1,512,128]{2,1,0:T(8,128)(2,1)S(1)} all-gather(bf16[1,256,128]{2,1,0:T(8,128)(2,1)S(1)} %copy-done), channel_id=5, replica_groups=mesh['gx'=4,'gy'=4,'gz'=2] {'gz'}, dimensions={1}, use_global_device_ids=true | all-gather | bytes 196608 | tf_op jit(solution)/shard_map/all_gather | solution.py:47
  76.2 17.2 %all-gather.4 = bf16[1,2048,128]{2,1,0:T(8,128)(2,1)} all-gather(bf16[1,512,128]{2,1,0:T(8,128)(2,1)S(1)} %all-gather.3), channel_id=6, replica_groups=mesh['gx'=4,'gy'=4,'gz'=2] {'gy'}, dimensions={1}, use_global_device_ids=true | all-gather | bytes 655360 | tf_op jit(solution)/shard_map/all_gather | solution.py:53
  93.4 0.0 all-gather.22.cloned.1.call-update
  93.4 0.0 all-gather.32.cloned.1.call-start
  93.5 30.7 %all-gather.30.cloned.1.call-done = bf16[1,512,2048]{2,1,0:T(8,128)(2,1)} async-done(((bf16[1,512,512]{2,1,0:T(8,128)(2,1)}), bf16[1,512,2048]{2,1,0:T(8,128)(2,1)}) %all-gather.30.cloned.1.call-update) | async-done | bytes 2097168 | tf_op jit(solution)/shard_map/all_gather | solution.py:68
  124.2 0.0 all-gather.32.cloned.1.call-update
  124.2 0.0 copy-done.3
  124.2 3.1 %all-gather = bf16[1,512]{1,0:T(2,128)(2,1)S(1)} all-gather(bf16[1,256]{1,0:T(2,128)(2,1)S(1)} %copy-done.3), channel_id=2, replica_groups=mesh['gx'=4,'gy'=4,'gz'=2] {'gz'}, dimensions={1}, use_global_device_ids=true | all-gather | bytes 1536 | tf_op jit(solution)/shard_map/all_gather | solution.py:44
  127.3 9.3 %all-gather.1 = bf16[1,2048]{1,0:T(2,128)(2,1)S(1)} all-gather(bf16[1,512]{1,0:T(2,128)(2,1)S(1)} %all-gather), channel_id=3, replica_groups=mesh['gx'=4,'gy'=4,'gz'=2] {'gy'}, dimensions={1}, use_global_device_ids=true | all-gather | bytes 5120 | tf_op jit(solution)/shard_map/all_gather | solution.py:50
  136.6 9.6 %all-gather.2 = bf16[1,8192]{1,0:T(2,128)(2,1)S(1)} all-gather(bf16[1,2048]{1,0:T(2,128)(2,1)S(1)} %all-gather.1), channel_id=4, replica_groups=mesh['gx'=4,'gy'=4,'gz'=2] {'gx'}, dimensions={1}, use_global_device_ids=true | all-gather | bytes 20480 | tf_op jit(solution)/shard_map/all_gather | solution.py:55
  146.2 0.0 copy-done.1
  146.3 3.1 %fusion.2 = f32[256]{0:T(256)S(1)} fusion(bf16[256,8192]{1,0:T(8,128)(2,1)} %param.8), kind=kLoop, calls=%fused_computation.5 | loop fusion | flops 6291200 | bytes 4195328 | tf_op jit(solution)/shard_map/reduce_sum | solution.py:41
  149.4 0.0 copy-done.2
  149.4 0.1 compare_and_fusion
  149.5 0.3 multiply_cosine_fusion
  149.8 0.0 all-gather.24.cloned.1.call-done
  149.9 4.6 %fusion.8 = f32[256,128]{0,1:T(8,128)S(1)} fusion(bf16[1,8192,128]{2,1,0:T(8,128)(2,1)} %all-gather.24.cloned.1.call-done, bf16[256,8192]{1,0:T(8,128)(2,1)} %param.8, f32[8192]{0:T(1024)S(1)} %bitcast.83, f32[256]{0:T(256)S(1)} %add_rsqrt_fusion), kind=kOutput, calls=%fused_computation.11 | convolution fusion | flops 545259520 | bytes 6456320 | tf_op jit(solution)/shard_map/dot_general | solution.py:61
  154.6 0.1 copy.10
  154.7 0.1 copy.9
  154.8 52.9 %all-gather.28.cloned.1.call-done = bf16[1,8192,512]{2,1,0:T(8,128)(2,1)} async-done(((bf16[1,2048,512]{2,1,0:T(8,128)(2,1)}), bf16[1,8192,512]{2,1,0:T(8,128)(2,1)}) %all-gather.28.cloned.1.call-update) | async-done | bytes 8388624 | tf_op jit(solution)/shard_map/all_gather | solution.py:56
  207.6 7.0 %fusion.6 = f32[256,512]{1,0:T(8,128)S(1)} fusion(bf16[1,8192,512]{2,1,0:T(8,128)(2,1)} %all-gather.28.cloned.1.call-done, bf16[256,8192]{1,0:T(8,128)(2,1)} %param.8, f32[8192]{0:T(1024)S(1)} %bitcast.84, f32[256]{0:T(256)S(1)} %add_rsqrt_fusion), kind=kOutput, calls=%fused_computation.9 | convolution fusion | flops 2155872256 | bytes 13140992 | tf_op jit(solution)/shard_map/dot_general | solution.py:60
  214.6 0.2 reshape.93
  214.8 0.3 slice_negate_fusion
  215.2 0.4 maximum_multiply_fusion
  215.5 0.1 mul.85
  215.6 0.5 fusion.44
  216.2 15.4 %all-gather.22.cloned.1.call-done = bf16[1,8192,128]{2,1,0:T(8,128)(2,1)} async-done(((bf16[1,2048,128]{2,1,0:T(8,128)(2,1)}), bf16[1,8192,128]{2,1,0:T(8,128)(2,1)}) %all-gather.22.cloned.1.call-update) | async-done | bytes 2097168 | tf_op jit(solution)/shard_map/all_gather | solution.py:58
  231.6 4.7 %convolution_convert_fusion = bf16[128,4,256]{2,0,1:T(8,128)(2,1)S(1)} fusion(bf16[1,8192,128]{2,1,0:T(8,128)(2,1)} %all-gather.22.cloned.1.call-done, f32[4,256,256]{1,2,0:T(8,128)S(1)} %get-tuple-element.15, f32[4,256]{1,0:T(4,128)S(1)} %get-tuple-element.14, bf16[256,8192]{1,0:T(8,128)(2,1)} %param.8, f32[8192]{0:T(1024)S(1)} %bitcast.85, ...), kind=kOutput, calls=%fused_computation.20 | convolution fusion | flops 613056512 | bytes 7640064 | tf_op jit(solution)/shard_map/hts,sd->thd/dot_general | solution.py:32
  236.3 55.1 %all-gather.32.cloned.1.call-done = bf16[1,512,8192]{2,1,0:T(8,128)(2,1)} async-done(((bf16[1,512,2048]{2,1,0:T(8,128)(2,1)}), bf16[1,512,8192]{2,1,0:T(8,128)(2,1)}) %all-gather.32.cloned.1.call-update) | async-done | bytes 8388624 | tf_op jit(solution)/shard_map/all_gather | solution.py:71
  291.3 9.0 %fusion.1 = bf16[256,8192]{1,0:T(8,128)(2,1)} fusion(bf16[256,512]{0,1:T(8,128)(2,1)S(1)} %bitcast.82, bf16[256,8192]{1,0:T(8,128)(2,1)} %param.8, bf16[1,512,8192]{2,1,0:T(8,128)(2,1)} %all-gather.32.cloned.1.call-done), kind=kOutput, calls=%fused_computation.4 | convolution fusion | flops 2153775104 | bytes 17039360 | tf_op jit(solution)/shard_map/dot_general | solution.py:69
  (7 shorter events, 0.1 us)
Async XLA Ops:
  6.5 65.9 %copy-start = (bf16[1,256,128]{2,1,0:T(8,128)(2,1)S(1)}, bf16[1,256,128]{2,1,0:T(8,128)(2,1)}, u32[]{:S(2)}) copy-start(bf16[1,256,128]{2,1,0:T(8,128)(2,1)} %param.14) | copy-start | bytes 196612
  6.5 65.8 %all-gather.26.cloned.1.call-start = ((), (), s32[]{:S(2)}) async-start(), calls=%async_computation.2 | async-start | bytes 2621440 | tf_op jit(solution)/shard_map/all_gather | solution.py:51
  17.4 106.8 %copy-start.3 = (bf16[1,256]{1,0:T(2,128)(2,1)S(1)}, bf16[1,256]{1,0:T(2,128)(2,1)}, u32[]{:S(2)}) copy-start(bf16[1,256]{1,0:T(2,128)(2,1)} %param.11) | copy-start | bytes 1540
  17.4 128.9 %copy-start.1 = (s32[256]{0:T(256)S(1)}, s32[256]{0:T(256)}, u32[]{:S(2)}) copy-start(s32[256]{0:T(256)} %param.10) | copy-start | bytes 3076
  17.4 106.8 %all-gather.30.cloned.1.call-start = ((), (), s32[]{:S(2)}) async-start(), calls=%async_computation.4 | async-start | bytes 2621440 | tf_op jit(solution)/shard_map/all_gather | solution.py:68
  25.1 124.8 %all-gather.24.cloned.1.call-start = ((), (), s32[]{:S(2)}) async-start(), calls=%async_computation.1 | async-start | bytes 2621440 | tf_op jit(solution)/shard_map/all_gather | solution.py:57
  51.3 156.3 %all-gather.28.cloned.1.call-start = ((), (), s32[]{:S(2)}) async-start(), calls=%async_computation.3 | async-start | bytes 10485760 | tf_op jit(solution)/shard_map/all_gather | solution.py:56
  72.4 77.0 %copy-start.2 = (s32[256]{0:T(256)S(1)}, s32[256]{0:T(256)}, u32[]{:S(2)}) copy-start(s32[256]{0:T(256)} %param.9) | copy-start | bytes 3076
  72.4 159.2 %all-gather.22.cloned.1.call-start = ((), (), s32[]{:S(2)}) async-start(), calls=%async_computation | async-start | bytes 2621440 | tf_op jit(solution)/shard_map/all_gather | solution.py:58
  93.4 197.9 %all-gather.32.cloned.1.call-start = ((), (), s32[]{:S(2)}) async-start(), calls=%async_computation.5 | async-start | bytes 10485760 | tf_op jit(solution)/shard_map/all_gather | solution.py:71
Sparse Core Ops, SparseCore 0:
  17.5 54.8 all-gather.25
  73.9 50.2 all-gather.29
  125.7 22.0 all-gather.23
  149.3 58.2 all-gather.27
  209.0 22.5 all-gather.21
  233.0 58.2 all-gather.31
where the time goes:
time: 308 us; the launch traced here: 307 us
  waiting for transfers between devices  175 us (57%)
  blocking collectives  87.6 us (28%)
  matrix products  25.9 us (8%)
  between operations  13.6 us (4%)
  other arithmetic  4.35 us (1%)
    all_gather x1, waiting for transfers between devices, body(): lax.all_gather(middle_cols, 'gx', axis=1, tiled=True)  55.1 us
    all_gather x1, waiting for transfers between devices, body(): query_piece = lax.all_gather(middle[1], 'gx', axis=0, tiled=True)  52.9 us
    all_gather x1, waiting for transfers between devices, body(): middle_cols = lax.all_gather(inner_cols, 'gy', axis=1, tiled=True)  30.7 us
    all_gather x1, blocking collectives, body(): lax.all_gather(inner[2], 'gy', axis=0, tiled=True)  21.2 us
    all_gather x1, waiting for transfers between devices, body(): lax.all_gather(inner[1], 'gy', axis=0, tiled=True)  20.9 us
    all_gather x1, blocking collectives, body(): lax.all_gather(inner[3], 'gy', axis=0, tiled=True)  17.2 us
    all_gather x1, waiting for transfers between devices, body(): value_piece = lax.all_gather(middle[3], 'gx', axis=0, tiled=True)  15.4 us
    all_gather x1, blocking collectives, body(): lax.all_gather(q_weight[0], 'gz', axis=0, tiled=True)  10.8 us
  transfers between devices with their start and end apart: 6, of which 5 were waited for; matrix products, arithmetic and copies ran while one was open for 7% of the time, Pallas kernels for 0%

commit v1 on v0

v1 whole, which is shorter than its diff:
```python
import functools
import itertools
import math

import jax
import jax.numpy as jnp
from jax import lax
from jax.experimental import pallas as pl
from jax.experimental.pallas import tpu as pltpu
from jax.sharding import PartitionSpec as P

AXES = ("gx", "gy", "gz")
CORES = 2
MAX_RECEIVES = 256
ORDERS = ((0, 1, 2), (1, 0, 2), (2, 0, 1), (2, 1, 0))
SHARES = (1, 1, 3, 3)


def rotate(values, positions):
    width = values.shape[-1]
    half = width // 2
    freqs = jnp.exp(-math.log(500000.0) * jnp.arange(half, dtype=jnp.float32) * 2.0 / width)
    angles = positions.astype(jnp.float32)[:, None] * freqs[None, :]
    cosine = jnp.concatenate([jnp.cos(angles), jnp.cos(angles)], -1)[:, None, :]
    sine = jnp.concatenate([jnp.sin(angles), jnp.sin(angles)], -1)[:, None, :]
    turned = jnp.concatenate([-values[..., half:], values[..., :half]], -1)
    return values * cosine + turned * sine


def attend(queries, keys, values, segment_ids, positions):
    count = queries.shape[0]
    scores = jnp.einsum(
        "thd,sd->hts", queries, keys, preferred_element_type=jnp.float32
    ) / math.sqrt(keys.shape[-1])
    allowed = (segment_ids[:, None] == segment_ids[None, :]) & (
        positions[None, :] <= positions[:, None]
    )
    scores = jnp.where(allowed[None], scores, -1e30)
    peak = jnp.max(scores, -1, keepdims=True)
    expd = jnp.exp(scores - peak)
    probs = (expd / jnp.sum(expd, -1, keepdims=True)).astype(jnp.bfloat16)
    mixed = jnp.einsum("hts,sd->thd", probs, values, preferred_element_type=jnp.float32)
    return mixed.astype(jnp.bfloat16).reshape(count, -1)


def arrivals(size):
    return [sorted(range(size), key=lambda other: (abs(other - own), other)) for own in range(size)]


def pick(table, place):
    if len(set(table)) == 1:
        return table[0]
    value = jnp.int32(table[0])
    for index in range(1, len(table)):
        value = jnp.where(place == index, jnp.int32(table[index]), value)
    return value


def pieces_of(rows, unit):
    units = rows // unit
    total = sum(SHARES)
    runs, start, seen = [], 0, 0
    for share in SHARES:
        seen += share
        stop = units * seen // total * unit
        runs.append((start, stop))
        start = stop
    return runs


def program_order(dims, pieces):
    events = []
    for number, (tensor, order, _) in enumerate(pieces):
        for combo in itertools.product(*(range(size) for size in dims)):
            hops, late = 0, 0
            for place, axis in enumerate(order):
                hops += combo[axis]
                late = late * 8 + combo[order[2 - place]]
            if hops:
                events.append((tensor, hops, late, number, combo))
    events.sort()
    return [(number, combo) for _, _, _, number, combo in events]


class Gather:
    def __init__(self, dims, pieces, refs_in, refs_out, slices, own_sems, send_sem, recv_sem, cross_sem):
        self.dims, self.pieces = dims, pieces
        self.refs_in, self.refs_out, self.slices = refs_in, refs_out, slices
        self.send_sem, self.recv_sem, self.cross_sem = send_sem, recv_sem, cross_sem
        gx, gy, gz = (lax.axis_index(name) for name in AXES)
        self.core = lax.rem(gx, CORES)
        self.me = (gz, lax.div(gx, CORES), gy)
        self.tables = [arrivals(size) for size in dims]
        self.sends = 0
        self.pending = []

    def device(self, place, core):
        x, y, z = place
        return (y * CORES + core, z, x)

    def line(self, place):
        x, y, z = place
        return (y * self.dims[2] + z) * self.dims[0] + x

    def block(self, place, core):
        x, y, z = place
        return ((y * CORES + core) * self.dims[2] + z) * self.dims[0] + x

    def neighbour(self, axis, step):
        place = list(self.me)
        place[axis] = place[axis] + step
        return tuple(place)

    def other(self, axis):
        place = list(self.me)
        place[axis] = 1 - place[axis]
        return tuple(place)

    def barrier(self):
        sem = pltpu.get_barrier_semaphore()
        mesh = pl.DeviceIdType.MESH
        count = 1
        pl.semaphore_signal(sem, inc=1, device_id=self.device(self.me, 1 - self.core), device_id_type=mesh)
        for axis, size in enumerate(self.dims):
            if size == 2:
                pl.semaphore_signal(
                    sem, inc=1, device_id=self.device(self.other(axis), self.core), device_id_type=mesh
                )
                count = count + 1
            elif size > 2:
                for step in (-1, 1):
                    inside = self.inside(axis, step)

                    @pl.when(inside)
                    def _(axis=axis, step=step):
                        pl.semaphore_signal(
                            sem,
                            inc=1,
                            device_id=self.device(self.neighbour(axis, step), self.core),
                            device_id_type=mesh,
                        )

                    count = count + inside.astype(jnp.int32)
        pl.semaphore_wait(sem, count)

    def inside(self, axis, step):
        return self.me[axis] > 0 if step < 0 else self.me[axis] < self.dims[axis] - 1

    def source(self, number, owner, own):
        tensor = self.pieces[number][0]
        if own:
            return self.slices[tensor](self.refs_in[tensor], None, self.pieces[number][2])
        return self.slices[tensor](self.refs_out[tensor], self.block(owner, self.core), self.pieces[number][2])

    def copy(self, number, owner, own, device, sem, cross=False):
        tensor = self.pieces[number][0]
        target = self.slices[tensor](self.refs_out[tensor], self.block(owner, self.core), self.pieces[number][2])
        landed = self.cross_sem if cross else self.recv_sem
        return pltpu.make_async_remote_copy(
            src_ref=self.source(number, owner, own),
            dst_ref=target,
            send_sem=self.send_sem.at[sem],
            recv_sem=landed.at[number, self.line(owner)],
            device_id=device,
            device_id_type=pl.DeviceIdType.MESH,
        )

    def send(self, number, owner, own, place, condition=None, cross=False):
        sem = self.sends
        self.sends += 1
        core = 1 - self.core if cross else self.core

        def make():
            return self.copy(number, owner, own, self.device(place, core), sem, cross)

        if condition is None:
            make().start()
        else:
            pl.when(condition)(lambda: make().start())
        self.pending.append((make, condition))

    def pass_on(self, number, combo):
        order = self.pieces[number][1]
        owner = tuple(
            pick([row[index] for row in table], here)
            for table, index, here in zip(self.tables, combo, self.me)
        )
        own = not any(combo)
        last = max((place for place, axis in enumerate(order) if combo[axis]), default=-1)
        if last >= 0:
            axis = order[last]
            if self.dims[axis] > 2:
                up = owner[axis] < self.me[axis]
                step = jnp.where(up, 1, -1)
                goes = jnp.where(up, self.me[axis] < self.dims[axis] - 1, self.me[axis] > 0)
                self.send(number, owner, own, self.neighbour(axis, step), goes)
        for axis in order[last + 1 :]:
            if self.dims[axis] == 2:
                self.send(number, owner, own, self.other(axis))
            elif self.dims[axis] > 2:
                for step in (-1, 1):
                    self.send(number, owner, own, self.neighbour(axis, step), self.inside(axis, step))
        self.send(number, owner, own, self.me, cross=True)

    def take(self, number, combo, cross=False):
        owner = tuple(
            pick([row[index] for row in table], here)
            for table, index, here in zip(self.tables, combo, self.me)
        )
        tensor = self.pieces[number][0]
        core = 1 - self.core if cross else self.core
        landed = self.slices[tensor](self.refs_out[tensor], self.block(owner, core), self.pieces[number][2])
        sem = self.cross_sem if cross else self.recv_sem
        pltpu.make_async_copy(landed, landed, sem.at[number, self.line(owner)]).wait()

    def drain(self):
        for make, condition in self.pending:
            if condition is None:
                make().wait_send()
            else:
                pl.when(condition)(lambda make=make: make().wait_send())


def gather_kernel(dims, pieces, order, w_ref, o_ref, wf_ref, of_ref, own_sem, send_sem, recv_sem, cross_sem):
    rows = w_ref.shape[0]
    cols = o_ref.shape[1]

    def w_slice(ref, block, run):
        start = run[0] if block is None else block * rows + run[0]
        if block is not None:
            start = pl.multiple_of(start, 16)
        return ref.at[pl.ds(start, run[1] - run[0]), :]

    def o_slice(ref, block, run):
        if block is None:
            return ref.at[pl.ds(run[0], run[1] - run[0]), :]
        return ref.at[pl.ds(run[0], run[1] - run[0]), pl.ds(pl.multiple_of(block * cols, cols), cols)]

    g = Gather(dims, pieces, (w_ref, o_ref), (wf_ref, of_ref), (w_slice, o_slice), own_sem, send_sem, recv_sem, cross_sem)
    mine = g.block(g.me, g.core)
    keep_w = pltpu.make_async_copy(w_ref, w_slice(wf_ref, mine, (0, rows)), own_sem.at[0])
    keep_o = pltpu.make_async_copy(o_ref, o_slice(of_ref, mine, (0, o_ref.shape[0])), own_sem.at[1])
    g.barrier()
    keep_w.start()
    keep_o.start()
    zero = (0, 0, 0)
    for number, piece in enumerate(pieces):
        if piece[0] == 0:
            g.pass_on(number, zero)
    weights = sum(1 for number, _ in order if pieces[number][0] == 0)
    for index, (number, combo) in enumerate(order):
        if index == weights // 2:
            for later, piece in enumerate(pieces):
                if piece[0] == 1:
                    g.pass_on(later, zero)
        g.take(number, combo)
        g.pass_on(number, combo)
    for number, combo in [(number, zero) for number in range(len(pieces))] + list(order):
        g.take(number, combo, cross=True)
    g.drain()
    keep_w.wait()
    keep_o.wait()


def count_sends(dims, pieces):
    total = 0
    for _, order, _ in pieces:
        for combo in itertools.product(*(range(size) for size in dims)):
            last = max((place for place, axis in enumerate(order) if combo[axis]), default=-1)
            if last >= 0 and dims[order[last]] > 2:
                total += 1
            total += sum(min(dims[axis] - 1, 2) for axis in order[last + 1 :]) + 1
    return total


def gather_all(dims, weight, out_weight):
    rows, width = weight.shape
    depth, cols = out_weight.shape
    count = math.prod(dims) * CORES
    pieces = [(0, order, run) for order, run in zip(ORDERS, pieces_of(rows, 16))]
    pieces += [(1, order, run) for order, run in zip(ORDERS, pieces_of(depth, 16))]
    pieces = [piece for piece in pieces if piece[2][1] > piece[2][0]]
    order = program_order(dims, pieces)
    lines = math.prod(dims)
    return pl.pallas_call(
        functools.partial(gather_kernel, dims, pieces, order),
        out_shape=(
            jax.ShapeDtypeStruct((count * rows, width), weight.dtype),
            jax.ShapeDtypeStruct((depth, count * cols), out_weight.dtype),
        ),
        in_specs=[pl.BlockSpec(memory_space=pl.ANY)] * 2,
        out_specs=[pl.BlockSpec(memory_space=pl.ANY)] * 2,
        scratch_shapes=[
            pltpu.SemaphoreType.DMA((2,)),
            pltpu.SemaphoreType.DMA((count_sends(dims, pieces),)),
            pltpu.SemaphoreType.DMA((len(pieces), lines)),
            pltpu.SemaphoreType.DMA((len(pieces), lines)),
        ],
        compiler_params=pltpu.CompilerParams(collective_id=0, has_side_effects=True),
    )(weight, out_weight)


def body(dims, stream, segment_ids, positions, norm_gain, q_weight, k_weight, v_weight, o_weight):
    count = stream.shape[0]
    head_size = k_weight.shape[2]
    queries_width = q_weight.shape[2]
    widened = stream.astype(jnp.float32)
    inverse = lax.rsqrt(jnp.mean(widened * widened, -1, keepdims=True) + 1e-05)
    joined = jnp.concatenate([q_weight[0], k_weight[0], v_weight[0]], -1).astype(jnp.float32)
    weight = (joined * norm_gain[0].astype(jnp.float32)[:, None]).astype(jnp.bfloat16)
    if CORES * len(ORDERS) * math.prod(dims) <= MAX_RECEIVES:
        full, out_full = gather_all(dims, weight, o_weight[0])
    else:
        full, out_full = weight, o_weight[0]
        for name in reversed(AXES):
            full = lax.all_gather(full, name, axis=0, tiled=True)
            out_full = lax.all_gather(out_full, name, axis=1, tiled=True)
    raw = jnp.dot(stream, full, preferred_element_type=jnp.float32) * inverse
    query_raw = raw[:, :queries_width]
    key_raw = raw[:, queries_width : queries_width + head_size]
    value_raw = raw[:, queries_width + head_size :]
    queries = rotate(query_raw.reshape(count, -1, head_size), positions).astype(jnp.bfloat16)
    keys = rotate(key_raw[:, None, :], positions)[:, 0, :].astype(jnp.bfloat16)
    values = value_raw.astype(jnp.bfloat16)
    mixed = attend(queries, keys, values, segment_ids, positions)
    branch = jnp.dot(mixed, out_full, preferred_element_type=jnp.float32)
    return (widened + branch).astype(jnp.bfloat16)


def solution(mesh):
    tokens = AXES
    in_specs = (
        P(tokens, None),
        P(tokens),
        P(tokens),
        P(None, tokens),
        P(None, tokens, None),
        P(None, tokens, None),
        P(None, tokens, None),
        P(None, None, tokens),
    )
    dims = (mesh.shape["gz"], mesh.shape["gx"] // CORES, mesh.shape["gy"])
    return jax.shard_map(
        functools.partial(body, dims),
        mesh=mesh,
        in_specs=in_specs,
        out_specs=P(tokens, None),
        check_vma=False,
    )
```

time: 308 us -> 116 us (0.38)
  waiting for transfers between devices: 175 us -> 0 us
  Pallas kernels: 0 us -> 91 us
  blocking collectives: 87.6 us -> 0 us
  between operations: 13.6 us -> 0.14 us
  matrix products: 25.9 us -> 18.1 us
    all_gather x6 -> x0, waiting for transfers between devices: 175 us -> none  [the longest x1 55.1 us: body(): lax.all_gather(middle_cols, 'gx', axis=1, tiled=True)]
    pallas_call x0 -> x1, Pallas kernels: none -> 91 us  [gather_all(): pl.pallas_call(functools.partial(gather_kernel, dims, pieces, order), out...]
    all_gather x9 -> x0, blocking collectives: 87.6 us -> none  [the longest x1 21.2 us: body(): lax.all_gather(inner[2], 'gy', axis=0, tiled=True)]
    dot_general x1, matrix products: 4.67 us -> 0.41 us  [attend(): jnp.einsum('hts,sd->thd', probs, values, preferred_element_type=jnp.float32)]
    dot_general x3, matrix products: 20.7 us -> 17.1 us  [the longest x1 9.02 us: body(): branch = jnp.dot(mixed, out_full, preferred_element_type=jnp.float32)]
  transfers between devices with their start and end apart: 6 -> 0, of which waited for: 5 -> 0; matrix products, arithmetic and copies ran while one was open for 7% -> 0% of each run, Pallas kernels for 0% -> 0%
where the time goes in v1:
time: 116 us
  Pallas kernels  91 us (78%)
  matrix products  18.1 us (16%)
  other arithmetic  6.4 us (6%)
    pallas_call x1, Pallas kernels, gather_all(): pl.pallas_call(functools.partial(gather_kernel, dims, pieces, order), out...  91 us
    dot_general x1, matrix products, body(): branch = jnp.dot(mixed, out_full, preferred_element_type=jnp.float32)  9.02 us
    dot_general x1, matrix products, body(): raw = jnp.dot(stream, full, preferred_element_type=jnp.float32) * inverse  7.78 us
    reduce_sum x1, other arithmetic, body(): inverse = lax.rsqrt(jnp.mean(widened * widened, -1, keepdims=True) + 1e-05)  3.1 us

profile of v1, /device:TPU:1, one launch (start us, length us, event | category | flops | bytes accessed | tf_op | source)
XLA Modules:
  0.0 115.7 jit_solution(5805383065196029036)
XLA Ops:
  0.0 0.7 convert_element_type.60
  0.7 1.9 %multiply_convert_fusion.w_ref = bf16[256,768]{1,0:T(8,128)(2,1)} fusion(bf16[256,128]{1,0:T(8,128)(2,1)} %bitcast.54, bf16[256,128]{1,0:T(8,128)(2,1)} %bitcast.55, bf16[256,512]{1,0:T(8,128)(2,1)} %bitcast.52, f32[256]{0:T(256)S(1)} %bitcast.56), kind=kLoop, calls=%fused_computation.14 | loop fusion | flops 1572864 | bytes 787456 | tf_op jit(solution)/shard_map/convert_element_type | solution.py:310
  2.6 91.0 %shard_map.82 = (bf16[8192,768]{1,0:T(8,128)(2,1)}, bf16[512,8192]{1,0:T(8,128)(2,1)}) custom-call(bf16[256,768]{1,0:T(8,128)(2,1)} %multiply_convert_fusion.w_ref, bf16[512,256]{1,0:T(8,128)(2,1)} %bitcast.53), custom_call_target="tpu_custom_call" | custom-call | tf_op jit(solution)/shard_map/pallas_call | solution.py:285
  93.6 3.1 %fusion.2 = f32[256]{0:T(256)S(1)} fusion(bf16[256,8192]{1,0:T(8,128)(2,1)} %param.8), kind=kLoop, calls=%fused_computation.4 | loop fusion | flops 6291200 | bytes 4195328 | tf_op jit(solution)/shard_map/reduce_sum | solution.py:308
  96.8 0.0 copy-start
  96.8 0.0 copy-start.1
  96.8 7.8 %fusion.7 = f32[256,768]{0,1:T(8,128)S(1)} fusion(bf16[8192,768]{1,0:T(8,128)(2,1)} %get-tuple-element.7, bf16[256,8192]{1,0:T(8,128)(2,1)} %param.8, f32[256]{0:T(256)S(1)} %add_rsqrt_fusion), kind=kOutput, calls=%fused_computation.11 | convolution fusion | flops 3221422080 | bytes 17564672 | tf_op jit(solution)/shard_map/dot_general | solution.py:318
  104.6 0.0 copy-done
  104.6 0.3 multiply_cosine_fusion
  105.1 0.1 fusion.8
  105.2 0.0 copy-done.1
  105.3 0.1 compare_and_fusion
  105.4 0.3 fusion.6
  105.7 0.5 fusion.18
  106.2 0.4 convolution_convert_fusion
  106.7 9.0 %fusion.1 = bf16[256,8192]{1,0:T(8,128)(2,1)} fusion(bf16[256,512]{0,1:T(8,128)(2,1)S(1)} %bitcast.51, bf16[512,8192]{1,0:T(8,128)(2,1)} %get-tuple-element.8, bf16[256,8192]{1,0:T(8,128)(2,1)} %param.8), kind=kOutput, calls=%fused_computation.3 | convolution fusion | flops 2153775104 | bytes 17039360 | tf_op jit(solution)/shard_map/dot_general | solution.py:326
  (9 shorter events, 0.2 us)
Async XLA Ops:
  96.8 7.8 %copy-start = (s32[256]{0:T(256)S(1)}, s32[256]{0:T(256)}, u32[]{:S(2)}) copy-start(s32[256]{0:T(256)} %param.10) | copy-start | bytes 3076
  96.8 8.5 %copy-start.1 = (s32[256]{0:T(256)S(1)}, s32[256]{0:T(256)}, u32[]{:S(2)}) copy-start(s32[256]{0:T(256)} %param.9) | copy-start | bytes 3076

commit v2 on v1

--- a/solution.py
+++ b/solution.py
@@ -12,6 +12,9 @@
 AXES = ("gx", "gy", "gz")
 CORES = 2
 MAX_RECEIVES = 256
+STEP = 256
+LUMPS = 8
+VMEM_BYTES = 60 << 20
 ORDERS = ((0, 1, 2), (1, 0, 2), (2, 0, 1), (2, 1, 0))
 SHARES = (1, 1, 3, 3)
 
@@ -221,7 +224,50 @@
                 pl.when(condition)(lambda make=make: make().wait_send())
 
 
-def gather_kernel(dims, pieces, order, w_ref, o_ref, wf_ref, of_ref, own_sem, send_sem, recv_sem, cross_sem):
+def project(x_ref, wf_ref, acc_ref, lump):
+    steps = x_ref.shape[1] // STEP // LUMPS
+
+    @pl.loop(0, steps)
+    def _(index):
+        span = pl.ds(pl.multiple_of((lump * steps + index) * STEP, STEP), STEP)
+        acc_ref[...] += jnp.dot(x_ref[:, span], wf_ref[span, :], preferred_element_type=jnp.float32)
+
+
+def attend_local(x_ref, acc_ref, cos_ref, sin_ref, mask_ref, mixed_ref):
+    count, width = x_ref.shape
+    size = cos_ref.shape[1]
+    heads = mixed_ref.shape[1] // size
+
+    def squares(index, total):
+        part = x_ref[:, pl.ds(pl.multiple_of(index * STEP, STEP), STEP)].astype(jnp.float32)
+        return total + jnp.sum(part * part, -1, keepdims=True)
+
+    total = lax.fori_loop(0, width // STEP, squares, jnp.zeros((count, 1), jnp.float32))
+    inverse = lax.rsqrt(total / width + 1e-05)
+    cosine, sine = cos_ref[...], sin_ref[...]
+
+    def turned(head):
+        raw = acc_ref[:, head * size : (head + 1) * size] * inverse
+        return (raw * cosine + pltpu.roll(raw, size // 2, 1) * sine).astype(jnp.bfloat16)
+
+    keys = turned(heads)
+    values = (acc_ref[:, (heads + 1) * size :] * inverse).astype(jnp.bfloat16)
+    allowed = mask_ref[...] > 0.5
+    for head in range(heads):
+        scores = lax.dot_general(
+            turned(head), keys, (((1,), (1,)), ((), ())), preferred_element_type=jnp.float32
+        ) / math.sqrt(size)
+        scores = jnp.where(allowed, scores, -1e30)
+        expd = jnp.exp(scores - jnp.max(scores, -1, keepdims=True))
+        probs = (expd / jnp.sum(expd, -1, keepdims=True)).astype(jnp.bfloat16)
+        mixed = jnp.dot(probs, values, preferred_element_type=jnp.float32)
+        mixed_ref[:, head * size : (head + 1) * size] = mixed.astype(jnp.bfloat16)
+
+
+def gather_kernel(
+    dims, pieces, order, w_ref, o_ref, stream_ref, cos_ref, sin_ref, mask_ref, mixed_ref, of_ref,
+    wf_ref, x_ref, acc_ref, own_sem, send_sem, recv_sem, cross_sem,
+):
     rows = w_ref.shape[0]
     cols = o_ref.shape[1]
 
@@ -240,25 +286,42 @@
     mine = g.block(g.me, g.core)
     keep_w = pltpu.make_async_copy(w_ref, w_slice(wf_ref, mine, (0, rows)), own_sem.at[0])
     keep_o = pltpu.make_async_copy(o_ref, o_slice(of_ref, mine, (0, o_ref.shape[0])), own_sem.at[1])
+    fetch = pltpu.make_async_copy(stream_ref, x_ref, own_sem.at[2])
     g.barrier()
+    zero = (0, 0, 0)
+    numbers = list(range(len(pieces)))
+    for number in reversed(numbers):
+        if pieces[number][0] == 0:
+            g.pass_on(number, zero)
     keep_w.start()
     keep_o.start()
-    zero = (0, 0, 0)
-    for number, piece in enumerate(pieces):
-        if piece[0] == 0:
-            g.pass_on(number, zero)
+    fetch.start()
+    acc_ref[...] = jnp.zeros_like(acc_ref)
+    events = [(number, zero) for number in numbers] + list(order)
     weights = sum(1 for number, _ in order if pieces[number][0] == 0)
+    gap = max((len(order) - weights) // (2 * LUMPS), 1)
     for index, (number, combo) in enumerate(order):
         if index == weights // 2:
-            for later, piece in enumerate(pieces):
-                if piece[0] == 1:
+            for later in reversed(numbers):
+                if pieces[later][0] == 1:
                     g.pass_on(later, zero)
         g.take(number, combo)
         g.pass_on(number, combo)
-    for number, combo in [(number, zero) for number in range(len(pieces))] + list(order):
-        g.take(number, combo, cross=True)
+        since = index - weights
+        if since == gap:
+            for event in events:
+                if pieces[event[0]][0] == 0:
+                    g.take(*event, cross=True)
+            keep_w.wait()
+            fetch.wait()
+        if since >= gap and since % gap == 0 and since // gap <= LUMPS:
+            project(x_ref, wf_ref, acc_ref, since // gap - 1)
+        if since == gap * (LUMPS + 1):
+            attend_local(x_ref, acc_ref, cos_ref, sin_ref, mask_ref, mixed_ref)
+    for event in events:
+        if pieces[event[0]][0] == 1:
+            g.take(*event, cross=True)
     g.drain()
-    keep_w.wait()
     keep_o.wait()
 
 
@@ -273,7 +336,7 @@
     return total
 
 
-def gather_all(dims, weight, out_weight):
+def gather_all(dims, weight, out_weight, stream, cosine, sine, mask):
     rows, width = weight.shape
     depth, cols = out_weight.shape
     count = math.prod(dims) * CORES
@@ -285,19 +348,22 @@
     return pl.pallas_call(
         functools.partial(gather_kernel, dims, pieces, order),
         out_shape=(
-            jax.ShapeDtypeStruct((count * rows, width), weight.dtype),
+            jax.ShapeDtypeStruct((stream.shape[0], depth), stream.dtype),
             jax.ShapeDtypeStruct((depth, count * cols), out_weight.dtype),
         ),
-        in_specs=[pl.BlockSpec(memory_space=pl.ANY)] * 2,
-        out_specs=[pl.BlockSpec(memory_space=pl.ANY)] * 2,
+        in_specs=[pl.BlockSpec(memory_space=pl.ANY)] * 3 + [pl.BlockSpec(memory_space=pltpu.VMEM)] * 3,
+        out_specs=[pl.BlockSpec(memory_space=pltpu.VMEM), pl.BlockSpec(memory_space=pl.ANY)],
         scratch_shapes=[
-            pltpu.SemaphoreType.DMA((2,)),
+            pltpu.VMEM((count * rows, width), weight.dtype),
+            pltpu.VMEM(stream.shape, stream.dtype),
+            pltpu.VMEM((stream.shape[0], width), jnp.float32),
+            pltpu.SemaphoreType.DMA((3,)),
             pltpu.SemaphoreType.DMA((count_sends(dims, pieces),)),
             pltpu.SemaphoreType.DMA((len(pieces), lines)),
             pltpu.SemaphoreType.DMA((len(pieces), lines)),
         ],
-        compiler_params=pltpu.CompilerParams(collective_id=0, has_side_effects=True),
-    )(weight, out_weight)
+        compiler_params=pltpu.CompilerParams(collective_id=0, has_side_effects=True, vmem_limit_bytes=VMEM_BYTES),
+    )(weight, out_weight, stream, cosine, sine, mask)
 
 
 def body(dims, stream, segment_ids, positions, norm_gain, q_weight, k_weight, v_weight, o_weight):
@@ -305,24 +371,32 @@
     head_size = k_weight.shape[2]
     queries_width = q_weight.shape[2]
     widened = stream.astype(jnp.float32)
-    inverse = lax.rsqrt(jnp.mean(widened * widened, -1, keepdims=True) + 1e-05)
     joined = jnp.concatenate([q_weight[0], k_weight[0], v_weight[0]], -1).astype(jnp.float32)
     weight = (joined * norm_gain[0].astype(jnp.float32)[:, None]).astype(jnp.bfloat16)
     if CORES * len(ORDERS) * math.prod(dims) <= MAX_RECEIVES:
-        full, out_full = gather_all(dims, weight, o_weight[0])
+        half = head_size // 2
+        freqs = jnp.exp(-math.log(500000.0) * jnp.arange(half, dtype=jnp.float32) * 2.0 / head_size)
+        angles = positions.astype(jnp.float32)[:, None] * freqs[None, :]
+        cosine = jnp.concatenate([jnp.cos(angles), jnp.cos(angles)], -1)
+        sine = jnp.concatenate([-jnp.sin(angles), jnp.sin(angles)], -1)
+        allowed = (segment_ids[:, None] == segment_ids[None, :]) & (positions[None, :] <= positions[:, None])
+        mixed, out_full = gather_all(
+            dims, weight, o_weight[0], stream, cosine, sine, allowed.astype(jnp.float32)
+        )
     else:
         full, out_full = weight, o_weight[0]
         for name in reversed(AXES):
             full = lax.all_gather(full, name, axis=0, tiled=True)
             out_full = lax.all_gather(out_full, name, axis=1, tiled=True)
-    raw = jnp.dot(stream, full, preferred_element_type=jnp.float32) * inverse
-    query_raw = raw[:, :queries_width]
-    key_raw = raw[:, queries_width : queries_width + head_size]
-    value_raw = raw[:, queries_width + head_size :]
-    queries = rotate(query_raw.reshape(count, -1, head_size), positions).astype(jnp.bfloat16)
-    keys = rotate(key_raw[:, None, :], positions)[:, 0, :].astype(jnp.bfloat16)
-    values = value_raw.astype(jnp.bfloat16)
-    mixed = attend(queries, keys, values, segment_ids, positions)
+        inverse = lax.rsqrt(jnp.mean(widened * widened, -1, keepdims=True) + 1e-05)
+        raw = jnp.dot(stream, full, preferred_element_type=jnp.float32) * inverse
+        query_raw = raw[:, :queries_width]
+        key_raw = raw[:, queries_width : queries_width + head_size]
+        value_raw = raw[:, queries_width + head_size :]
+        queries = rotate(query_raw.reshape(count, -1, head_size), positions).astype(jnp.bfloat16)
+        keys = rotate(key_raw[:, None, :], positions)[:, 0, :].astype(jnp.bfloat16)
+        values = value_raw.astype(jnp.bfloat16)
+        mixed = attend(queries, keys, values, segment_ids, positions)
     branch = jnp.dot(mixed, out_full, preferred_element_type=jnp.float32)
     return (widened + branch).astype(jnp.bfloat16)
 

time: 116 us -> 112 us (0.966)
  matrix products: 18.1 us -> 9.03 us
  Pallas kernels: 91 us -> 96.3 us
    dot_general x3 -> x0, matrix products: 8.52 us -> none  [the longest x1 7.78 us: body(): raw = jnp.dot(stream, full, preferred_element_type=jnp.float32) * inverse]
    pallas_call x1, Pallas kernels: 91 us -> 96.3 us  [gather_all(): pl.pallas_call(functools.partial(gather_kernel, dims, pieces, order), out...]
    reduce_sum x1 -> x0, other arithmetic: 3.1 us -> none  [body(): inverse = lax.rsqrt(jnp.mean(widened * widened, -1, keepdims=True) + 1e-05)]
    convert_element_type x2, other arithmetic: 0.11 us -> 2.29 us  [the longest x1 1.61 us: body(): allowed.astype(jnp.float32)]
where the time goes in v2:
time: 112 us
  Pallas kernels  96.3 us (86%)
  matrix products  9.03 us (8%)
  other arithmetic  6.28 us (6%)
    pallas_call x1, Pallas kernels, gather_all(): pl.pallas_call(functools.partial(gather_kernel, dims, pieces, order), out...  96.3 us
    dot_general x1, matrix products, body(): branch = jnp.dot(mixed, out_full, preferred_element_type=jnp.float32)  9.03 us

profile of v2, /device:TPU:1, one launch (start us, length us, event | category | flops | bytes accessed | tf_op | source)
XLA Modules:
  0.0 111.7 jit_solution(15813920093001844269)
XLA Ops:
  0.0 0.7 convert_element_type.36
  0.7 0.7 convert_element_type.33
  1.4 1.6 %and_convert_fusion.mask_ref = f32[256,256]{1,0:T(8,128)} fusion(s32[256]{0:T(256)} %param.10, s32[256]{0:T(256)} %param.9), kind=kLoop, calls=%fused_computation.3 | loop fusion | flops 262144 | bytes 264192 | tf_op jit(solution)/shard_map/convert_element_type | solution.py:384
  3.0 0.5 fusion.1
  3.5 0.9 pad_maximum_fusion
  4.4 1.9 %multiply_convert_fusion.w_ref = bf16[256,768]{1,0:T(8,128)(2,1)} fusion(bf16[256,128]{1,0:T(8,128)(2,1)} %bitcast.9, bf16[256,128]{1,0:T(8,128)(2,1)} %bitcast.10, bf16[256,512]{1,0:T(8,128)(2,1)} %bitcast.7, f32[256]{0:T(256)S(1)} %bitcast.11), kind=kLoop, calls=%fused_computation.2 | loop fusion | flops 1572864 | bytes 787456 | tf_op jit(solution)/shard_map/convert_element_type | solution.py:375
  6.3 96.3 %shard_map.82 = (bf16[256,512]{1,0:T(8,128)(2,1)}, bf16[512,8192]{1,0:T(8,128)(2,1)}) custom-call(bf16[256,768]{1,0:T(8,128)(2,1)} %multiply_convert_fusion.w_ref, bf16[512,256]{1,0:T(8,128)(2,1)} %bitcast.8, bf16[256,8192]{1,0:T(8,128)(2,1)} %stream_ref.1, f32[256,128]{1,0:T(8,128)} %get-tuple-element.12.cos_ref, f32[256,128]{1,0:T(8,128)} %get-tuple-element.13.sin_ref, ...), custom_call_target="tpu_custom_call" | custom-call | tf_op jit(solution)/shard_map/pallas_call | solution.py:348
  102.6 9.0 %fusion = bf16[256,8192]{1,0:T(8,128)(2,1)} fusion(bf16[256,512]{1,0:T(8,128)(2,1)} %get-tuple-element.7, bf16[512,8192]{1,0:T(8,128)(2,1)} %get-tuple-element.8, bf16[256,8192]{1,0:T(8,128)(2,1)} %stream_ref.1), kind=kOutput, calls=%fused_computation.1 | convolution fusion | flops 2153775104 | bytes 17039360 | tf_op jit(solution)/shard_map/dot_general | solution.py:400
  (1 shorter events, 0.0 us)

commit v3 on v2

--- a/solution.py
+++ b/solution.py
@@ -16,7 +16,7 @@
 LUMPS = 8
 VMEM_BYTES = 60 << 20
 ORDERS = ((0, 1, 2), (1, 0, 2), (2, 0, 1), (2, 1, 0))
-SHARES = (1, 1, 3, 3)
+SHARES = (1, 1, 4, 4)
 
 
 def rotate(values, positions):
@@ -301,7 +301,7 @@
     weights = sum(1 for number, _ in order if pieces[number][0] == 0)
     gap = max((len(order) - weights) // (2 * LUMPS), 1)
     for index, (number, combo) in enumerate(order):
-        if index == weights // 2:
+        if index == weights * 4 // 5:
             for later in reversed(numbers):
                 if pieces[later][0] == 1:
                     g.pass_on(later, zero)

time: 112 us -> 112 us (level)
  no operation moved by 1% of the time
where the time goes in v3:
time: 112 us
  Pallas kernels  96.5 us (86%)
  matrix products  9.03 us (8%)
  other arithmetic  6.28 us (6%)
    pallas_call x1, Pallas kernels, gather_all(): pl.pallas_call(functools.partial(gather_kernel, dims, pieces, order), out...  96.5 us
    dot_general x1, matrix products, body(): branch = jnp.dot(mixed, out_full, preferred_element_type=jnp.float32)  9.03 us

profile of v3, /device:TPU:1, one launch (start us, length us, event | category | flops | bytes accessed | tf_op | source)
XLA Modules:
  0.0 111.8 jit_solution(16236363383899724798)
XLA Ops:
  0.0 0.7 convert_element_type.36
  0.7 0.7 convert_element_type.33
  1.4 1.6 %and_convert_fusion.mask_ref = f32[256,256]{1,0:T(8,128)} fusion(s32[256]{0:T(256)} %param.10, s32[256]{0:T(256)} %param.9), kind=kLoop, calls=%fused_computation.3 | loop fusion | flops 262144 | bytes 264192 | tf_op jit(solution)/shard_map/convert_element_type | solution.py:384
  3.0 0.5 fusion.1
  3.5 0.9 pad_maximum_fusion
  4.4 1.9 %multiply_convert_fusion.w_ref = bf16[256,768]{1,0:T(8,128)(2,1)} fusion(bf16[256,128]{1,0:T(8,128)(2,1)} %bitcast.9, bf16[256,128]{1,0:T(8,128)(2,1)} %bitcast.10, bf16[256,512]{1,0:T(8,128)(2,1)} %bitcast.7, f32[256]{0:T(256)S(1)} %bitcast.11), kind=kLoop, calls=%fused_computation.2 | loop fusion | flops 1572864 | bytes 787456 | tf_op jit(solution)/shard_map/convert_element_type | solution.py:375
  6.3 96.5 %shard_map.82 = (bf16[256,512]{1,0:T(8,128)(2,1)}, bf16[512,8192]{1,0:T(8,128)(2,1)}) custom-call(bf16[256,768]{1,0:T(8,128)(2,1)} %multiply_convert_fusion.w_ref, bf16[512,256]{1,0:T(8,128)(2,1)} %bitcast.8, bf16[256,8192]{1,0:T(8,128)(2,1)} %stream_ref.1, f32[256,128]{1,0:T(8,128)} %get-tuple-element.12.cos_ref, f32[256,128]{1,0:T(8,128)} %get-tuple-element.13.sin_ref, ...), custom_call_target="tpu_custom_call" | custom-call | tf_op jit(solution)/shard_map/pallas_call | solution.py:348
  102.8 9.0 %fusion = bf16[256,8192]{1,0:T(8,128)(2,1)} fusion(bf16[256,512]{1,0:T(8,128)(2,1)} %get-tuple-element.7, bf16[512,8192]{1,0:T(8,128)(2,1)} %get-tuple-element.8, bf16[256,8192]{1,0:T(8,128)(2,1)} %stream_ref.1), kind=kOutput, calls=%fused_computation.1 | convolution fusion | flops 2153775104 | bytes 17039360 | tf_op jit(solution)/shard_map/dot_general | solution.py:400
  (1 shorter events, 0.0 us)
